TPU v7x, 32 devices: a whole 2x2x4 slice. The times are simulated.
32 devices in a mesh: dp: 8 (over y, x, core), mp: 4 (over z).
Axes of the slice: x: 2, y: 2, z: 4, core: 2. Of those that a mesh axis runs over, the one named last changes fastest.
Arguments:
- feature_ids: int32 [8, 2048, 8], P('dp'), may hold values from 0 to 4095
- tables: bfloat16 [8, 4096, 128], P('dp'), may hold values from -5 to 5
- table_of_feature: int32 [8], replicated, may hold values from 0 to 7, each once
- cross_down: bfloat16 [2, 1024, 512], P(None, 'mp'), may hold values from -0.1875 to 0.1875
- cross_up: bfloat16 [2, 1024, 512], P(None, 'mp'), may hold values from -0.125 to 0.125
- cross_bias: float32 [2, 1024], P(None, 'mp'), may hold values from -3 to 3
- tower_weight: bfloat16 [1024, 2048], P('dp', 'mp'), may hold values from -0.1875 to 0.1875
- tower_bias: float32 [2048], P('mp'), may hold values from -3 to 3
Outputs:
- hidden: bfloat16 [2048, 2048], P('dp', 'mp')
Inputs may be any that keep to these rules, and one draw needn't show every extreme that they name: `feature_ids`: each id indexes a row of its own table. `table_of_feature`: each table serves exactly one feature.
All inputs are finite; a program needn't handle non-finite values.
Results may differ from a plain program's by a relative error of at most 0.015.
Values may be sent and summed in bfloat16 or wider, within the bound.
A program may use at most 64 MiB of HBM per device.

v0:
```python
import jax
import jax.numpy as jnp
from jax import lax
from jax.sharding import PartitionSpec as P


def body(
    feature_ids,
    tables,
    table_of_feature,
    cross_down,
    cross_up,
    cross_bias,
    tower_weight,
    tower_bias,
):
    groups = lax.axis_size("dp")
    members = lax.axis_size("mp")
    member = lax.axis_index("mp")
    table_count, batch_size, hot_count = feature_ids.shape
    row_count = batch_size // (groups * members)
    shaped = feature_ids[0].reshape(groups, members, row_count, hot_count)
    own_ids = lax.dynamic_index_in_dim(shaped, member, 1, keepdims=False).reshape(
        groups * row_count, hot_count
    )
    summed = jnp.zeros((groups * row_count, tables.shape[2]), jnp.float32)
    for hot_index in range(hot_count):
        summed = summed + jnp.take(tables[0], own_ids[:, hot_index], axis=0).astype(jnp.float32)
    columns = [summed.astype(jnp.bfloat16)]
    pooled = jnp.stack(columns, axis=1)
    regrouped = lax.all_to_all(pooled, "dp", split_axis=0, concat_axis=1, tiled=True)
    ordered = jnp.take(regrouped, table_of_feature, axis=1)
    by_width = lax.all_to_all(ordered, "mp", split_axis=1, concat_axis=0, tiled=True)
    group_rows = by_width.shape[0]
    embedded = by_width.reshape(group_rows, -1)
    embedded_wide = embedded.astype(jnp.float32)
    crossed = embedded
    layer_total = cross_down.shape[0]
    for layer_index in range(layer_total):
        partial_value = jnp.dot(
            crossed, cross_down[layer_index], preferred_element_type=jnp.float32
        )
        projected = lax.psum(partial_value.astype(jnp.bfloat16), "mp")
        lifted = lax.dot_general(
            projected,
            cross_up[layer_index],
            (((1,), (1,)), ((), ())),
            preferred_element_type=jnp.float32,
        )
        crossed = (
            embedded_wide * (lifted + cross_bias[layer_index]) + crossed.astype(jnp.float32)
        ).astype(jnp.bfloat16)
    full_rows = lax.all_gather(crossed, "mp", axis=1, tiled=True)
    pre_act = jnp.dot(
        full_rows,
        lax.all_gather(tower_weight, "dp", axis=0, tiled=True),
        preferred_element_type=jnp.float32,
    )
    return jax.nn.relu(pre_act + tower_bias).astype(jnp.bfloat16)


def solution(mesh):
    return jax.shard_map(
        body,
        mesh=mesh,
        in_specs=(
            P("dp", None, None),
            P("dp", None, None),
            P(),
            P(None, "mp", None),
            P(None, "mp", None),
            P(None, "mp"),
            P("dp", "mp"),
            P("mp"),
        ),
        out_specs=P("dp", "mp"),
        check_vma=False,
    )
```

profile of v0, /device:TPU:0, one launch (start us, length us, event | category | flops | bytes accessed | tf_op | source)
XLA Modules:
  0.0 143.6 jit_solution(9518459660529289800)
XLA Ops:
  7.4 1.0 reshape_squeeze.3
  8.8 1.3 gather_fusion.2
  10.2 1.3 gather_fusion.3
  11.5 1.3 gather_fusion.4
  12.9 1.3 gather_fusion.5
  14.2 1.3 gather_fusion.6
  15.6 1.3 gather_fusion.7
  17.0 1.3 gather_fusion.8
  18.3 1.3 gather_fusion.1
  19.7 0.8 fusion.16
  21.0 0.7 reduce.4
  21.7 0.7 reshape.125
  22.3 5.3 %all-to-all-start = ((bf16[8,2,4096]{2,1,0:T(2,128)(2,1)}), bf16[8,2,4096]{2,1,0:T(2,128)(2,1)S(1)}, u32[]{:S(2)}, u32[]{:S(2)}) async-start(bf16[8,2,4096]{2,1,0:T(2,128)(2,1)} %reshape.125), calls=%async_computation | async-start | bytes 262144 | tf_op jit(solution)/shard_map/all_to_all | solution.py:31
  27.8 5.4 %all-to-all-done = bf16[8,2,4096]{2,1,0:T(2,128)(2,1)S(1)} async-done(((bf16[8,2,4096]{2,1,0:T(2,128)(2,1)}), bf16[8,2,4096]{2,1,0:T(2,128)(2,1)S(1)}, u32[]{:S(2)}, u32[]{:S(2)}) %all-to-all-start) | async-done | bytes 131104 | tf_op jit(solution)/shard_map/all_to_all | solution.py:31
  34.0 10.6 %all_to_all.33 = bf16[64,8,128]{2,0,1:T(8,128)(2,1)S(1)} all-to-all(bf16[64,8,128]{2,0,1:T(8,128)(2,1)S(1)} %select_bitcast_fusion), channel_id=1, replica_groups=mesh['dp'=8,'mp'=4] {'mp'}, dimensions={1} | all-to-all | bytes 262144 | tf_op jit(solution)/shard_map/all_to_all | solution.py:33
  44.8 0.9 convolution_convert_fusion.1
  45.8 0.6 copy-done.2
  46.4 32.4 %all-reduce.3.cloned.1.call-done = bf16[256,512]{1,0:T(8,128)(2,1)} async-done(((bf16[256,512]{1,0:T(8,128)(2,1)}), bf16[256,512]{1,0:T(8,128)(2,1)}) %all-reduce.3.cloned.1.call-update) | async-done | bytes 262160 | tf_op jit(solution)/shard_map/psum | solution.py:43
  78.8 1.2 fusion.6
  80.0 0.9 convolution_convert_fusion
  81.5 35.1 %all-reduce.5.cloned.1.call-done = bf16[256,512]{1,0:T(8,128)(2,1)} async-done(((bf16[256,512]{1,0:T(8,128)(2,1)}), bf16[256,512]{1,0:T(8,128)(2,1)}) %all-reduce.5.cloned.1.call-update) | async-done | bytes 262160 | tf_op jit(solution)/shard_map/psum | solution.py:43
  116.6 1.2 fusion.7
  117.8 16.0 %all_gather.6 = bf16[256,1024]{1,0:T(8,128)(2,1)S(1)} all-gather(bf16[256,256]{1,0:T(8,128)(2,1)S(1)} %fusion.7), channel_id=1, replica_groups=mesh['dp'=8,'mp'=4] {'mp'}, dimensions={1}, use_global_device_ids=true | all-gather | bytes 655360 | tf_op jit(solution)/shard_map/all_gather | solution.py:53
  133.8 2.4 %fusion.1 = bf16[256,512]{1,0:T(8,128)(2,1)} fusion(bf16[256,1024]{1,0:T(8,128)(2,1)S(1)} %all_gather.6, bf16[1024,512]{1,0:T(8,128)(2,1)} %all-gather.2.cloned.1.call-done, f32[512]{0:T(512)S(1)} %copy-done.4), kind=kOutput, calls=%fused_computation.11 | convolution fusion | flops 268828672 | bytes 1837056 | tf_op jit(solution)/shard_map/dot_general | solution.py:54
  (51 shorter events, 2.5 us)
Async XLA Ops:
  7.4 1.4 %copy-start = (bf16[1,4096,128]{2,1,0:T(8,128)(2,1)S(1)}, bf16[1,4096,128]{2,1,0:T(8,128)(2,1)}, u32[]{:S(2)}) copy-start(bf16[1,4096,128]{2,1,0:T(8,128)(2,1)} %param.11) | copy-start | bytes 3145732
  22.3 5.4 %copy-start.5 = (s32[8]{0:T(128)S(1)}, s32[8]{0:T(128)}, u32[]{:S(2)}) copy-start(s32[8]{0:T(128)} %param.12) | copy-start | bytes 100
  22.3 10.8 %all-to-all-start = ((bf16[8,2,4096]{2,1,0:T(2,128)(2,1)}), bf16[8,2,4096]{2,1,0:T(2,128)(2,1)S(1)}, u32[]{:S(2)}, u32[]{:S(2)}) async-start(bf16[8,2,4096]{2,1,0:T(2,128)(2,1)} %reshape.125), calls=%async_computation | async-start | bytes 262144 | tf_op jit(solution)/shard_map/all_to_all | solution.py:31
  27.7 51.1 %all-reduce.3.cloned.1.call-start = ((), (), s32[]{:S(2)}) async-start(), calls=%async_computation.2 | async-start | bytes 524288 | tf_op jit(solution)/shard_map/psum | solution.py:43
  33.3 11.5 %copy-start.1 = (bf16[2,256,512]{2,1,0:T(8,128)(2,1)S(1)}, bf16[2,256,512]{2,1,0:T(8,128)(2,1)}, u32[]{:S(2)}) copy-start(bf16[2,256,512]{2,1,0:T(8,128)(2,1)} %param.13) | copy-start | bytes 1572868
  44.8 34.0 %copy-start.3 = (bf16[2,256,512]{2,1,0:T(8,128)(2,1)S(1)}, bf16[2,256,512]{2,1,0:T(8,128)(2,1)}, u32[]{:S(2)}) copy-start(bf16[2,256,512]{2,1,0:T(8,128)(2,1)} %param.14) | copy-start | bytes 1572868
  45.7 0.7 copy-start.2
  45.8 70.8 %all-reduce.5.cloned.1.call-start = ((), (), s32[]{:S(2)}) async-start(), calls=%async_computation.3 | async-start | bytes 524288 | tf_op jit(solution)/shard_map/psum | solution.py:43
  81.0 52.8 %all-gather.2.cloned.1.call-start = ((), (), s32[]{:S(2)}) async-start(), calls=%async_computation.4 | async-start | bytes 1179648 | tf_op jit(solution)/shard_map/all_gather | solution.py:56
  117.8 16.0 %copy-start.4 = (f32[512]{0:T(512)S(1)}, f32[512]{0:T(512)}, u32[]{:S(2)}) copy-start(f32[512]{0:T(512)} %param.17) | copy-start | bytes 6148
Sparse Core Ops, SparseCore 0:
  45.9 32.8 all-reduce.2
  81.1 35.4 all-reduce.4
Sparse Core Ops, SparseCore 1:
  83.3 23.1 all-gather.1
where the time goes:
time: 144 us
  waiting for transfers between devices  73.4 us (51%)
  blocking collectives  26.6 us (18%)
  between operations  15.2 us (11%)
  local copies, waits for them, and re-layouts  14.7 us (10%)
  matrix products  6.65 us (5%)
  starting transfers between devices  5.45 us (4%)
  other arithmetic  1.66 us (1%)
    psum x2, waiting for transfers between devices, body(): projected = lax.psum(partial_value.astype(jnp.bfloat16), 'mp')  67.4 us
    all_gather x1, blocking collectives, body(): full_rows = lax.all_gather(crossed, 'mp', axis=1, tiled=True)  16 us
    gather x8, local copies, waits for them, and re-layouts, body(): jnp.take(tables[0], own_ids[:, hot_index], axis=0).astype(jnp.float32)  10.7 us
    all_to_all x1, blocking collectives, body(): lax.all_to_all(ordered, 'mp', split_axis=1, concat_axis=0, tiled=True)  10.6 us
    all_to_all x1, waiting for transfers between devices, body(): lax.all_to_all(pooled, 'dp', split_axis=0, concat_axis=1, tiled=True)  5.4 us
    all_to_all x1, starting transfers between devices, body(): lax.all_to_all(pooled, 'dp', split_axis=0, concat_axis=1, tiled=True)  5.33 us
  transfers between devices with their start and end apart: 4, of which 3 were waited for; matrix products, arithmetic and copies ran while one was open for 1% of the time, Pallas kernels for 0%

commit v1 on v0

--- a/solution.py
+++ b/solution.py
@@ -30,7 +30,10 @@
     pooled = jnp.stack(columns, axis=1)
     regrouped = lax.all_to_all(pooled, "dp", split_axis=0, concat_axis=1, tiled=True)
     ordered = jnp.take(regrouped, table_of_feature, axis=1)
-    by_width = lax.all_to_all(ordered, "mp", split_axis=1, concat_axis=0, tiled=True)
+    by_width = jnp.concatenate(
+        lax.all_to_all(jnp.stack(jnp.split(ordered, lax.axis_size("mp"), axis=1)), "mp", 0, 0),
+        axis=0,
+    )
     group_rows = by_width.shape[0]
     embedded = by_width.reshape(group_rows, -1)
     embedded_wide = embedded.astype(jnp.float32)

time: 144 us -> 144 us (level)
  no operation moved by 1% of the time
where the time goes in v1:
time: 144 us
  waiting for transfers between devices  73.3 us (51%)
  blocking collectives  26.7 us (19%)
  between operations  15.2 us (11%)
  local copies, waits for them, and re-layouts  14.7 us (10%)
  matrix products  6.66 us (5%)
  starting transfers between devices  5.45 us (4%)
  other arithmetic  1.68 us (1%)
    psum x2, waiting for transfers between devices, body(): projected = lax.psum(partial_value.astype(jnp.bfloat16), 'mp')  67.4 us
    all_gather x1, blocking collectives, body(): full_rows = lax.all_gather(crossed, 'mp', axis=1, tiled=True)  16 us
    all_to_all x1, blocking collectives, body(): lax.all_to_all(jnp.stack(jnp.split(ordered, lax.axis_size('mp'), axis=1))...  10.8 us
    gather x8, local copies, waits for them, and re-layouts, body(): jnp.take(tables[0], own_ids[:, hot_index], axis=0).astype(jnp.float32)  10.7 us
    all_to_all x1, waiting for transfers between devices, body(): lax.all_to_all(pooled, 'dp', split_axis=0, concat_axis=1, tiled=True)  5.4 us
    all_to_all x1, starting transfers between devices, body(): lax.all_to_all(pooled, 'dp', split_axis=0, concat_axis=1, tiled=True)  5.33 us
  transfers between devices with their start and end apart: 4, of which 3 were waited for; matrix products, arithmetic and copies ran while one was open for 1% of the time, Pallas kernels for 0%

profile of v1, /device:TPU:0, one launch (start us, length us, event | category | flops | bytes accessed | tf_op | source)
XLA Modules:
  0.0 143.8 jit_solution(15382437378141541168)
XLA Ops:
  7.4 1.0 reshape_squeeze.3
  8.8 1.3 gather_fusion.2
  10.2 1.3 gather_fusion.3
  11.5 1.3 gather_fusion.4
  12.9 1.3 gather_fusion.5
  14.2 1.3 gather_fusion.6
  15.6 1.3 gather_fusion.7
  17.0 1.3 gather_fusion.8
  18.3 1.3 gather_fusion.1
  19.7 0.8 fusion.16
  21.0 0.7 reduce.4
  21.7 0.7 reshape.120
  22.3 5.3 %all-to-all-start = ((bf16[8,2,4096]{2,1,0:T(2,128)(2,1)}), bf16[8,2,4096]{2,1,0:T(2,128)(2,1)S(1)}, u32[]{:S(2)}, u32[]{:S(2)}) async-start(bf16[8,2,4096]{2,1,0:T(2,128)(2,1)} %reshape.120), calls=%async_computation | async-start | bytes 262144 | tf_op jit(solution)/shard_map/all_to_all | solution.py:31
  27.8 5.4 %all-to-all-done = bf16[8,2,4096]{2,1,0:T(2,128)(2,1)S(1)} async-done(((bf16[8,2,4096]{2,1,0:T(2,128)(2,1)}), bf16[8,2,4096]{2,1,0:T(2,128)(2,1)S(1)}, u32[]{:S(2)}, u32[]{:S(2)}) %all-to-all-start) | async-done | bytes 131104 | tf_op jit(solution)/shard_map/all_to_all | solution.py:31
  34.1 10.8 %all_to_all.23 = bf16[4,64,2,128]{3,1,2,0:T(8,128)(2,1)S(1)} all-to-all(bf16[4,64,2,128]{3,1,2,0:T(8,128)(2,1)S(1)} %pad_maximum_fusion), channel_id=1, replica_groups=mesh['dp'=8,'mp'=4] {'mp'}, dimensions={0} | all-to-all | bytes 262144 | tf_op jit(solution)/shard_map/all_to_all | solution.py:34
  45.0 0.9 convolution_convert_fusion.1
  46.0 0.6 copy-done.2
  46.6 32.3 %all-reduce.3.cloned.1.call-done = bf16[256,512]{1,0:T(8,128)(2,1)} async-done(((bf16[256,512]{1,0:T(8,128)(2,1)}), bf16[256,512]{1,0:T(8,128)(2,1)}) %all-reduce.3.cloned.1.call-update) | async-done | bytes 262160 | tf_op jit(solution)/shard_map/psum | solution.py:46
  79.0 1.2 fusion.6
  80.2 0.9 convolution_convert_fusion
  81.7 35.0 %all-reduce.5.cloned.1.call-done = bf16[256,512]{1,0:T(8,128)(2,1)} async-done(((bf16[256,512]{1,0:T(8,128)(2,1)}), bf16[256,512]{1,0:T(8,128)(2,1)}) %all-reduce.5.cloned.1.call-update) | async-done | bytes 262160 | tf_op jit(solution)/shard_map/psum | solution.py:46
  116.8 1.2 fusion.7
  118.0 16.0 %all_gather.6 = bf16[256,1024]{1,0:T(8,128)(2,1)S(1)} all-gather(bf16[256,256]{1,0:T(8,128)(2,1)S(1)} %fusion.7), channel_id=1, replica_groups=mesh['dp'=8,'mp'=4] {'mp'}, dimensions={1}, use_global_device_ids=true | all-gather | bytes 655360 | tf_op jit(solution)/shard_map/all_gather | solution.py:56
  134.0 2.4 %fusion.1 = bf16[256,512]{1,0:T(8,128)(2,1)} fusion(bf16[256,1024]{1,0:T(8,128)(2,1)S(1)} %all_gather.6, bf16[1024,512]{1,0:T(8,128)(2,1)} %all-gather.2.cloned.1.call-done, f32[512]{0:T(512)S(1)} %copy-done.4), kind=kOutput, calls=%fused_computation.11 | convolution fusion | flops 268828672 | bytes 1837056 | tf_op jit(solution)/shard_map/dot_general | solution.py:57
  (53 shorter events, 2.5 us)
Async XLA Ops:
  7.4 1.4 %copy-start = (bf16[1,4096,128]{2,1,0:T(8,128)(2,1)S(1)}, bf16[1,4096,128]{2,1,0:T(8,128)(2,1)}, u32[]{:S(2)}) copy-start(bf16[1,4096,128]{2,1,0:T(8,128)(2,1)} %param.11) | copy-start | bytes 3145732
  22.3 5.4 %copy-start.5 = (s32[8]{0:T(128)S(1)}, s32[8]{0:T(128)}, u32[]{:S(2)}) copy-start(s32[8]{0:T(128)} %param.12) | copy-start | bytes 100
  22.3 10.8 %all-to-all-start = ((bf16[8,2,4096]{2,1,0:T(2,128)(2,1)}), bf16[8,2,4096]{2,1,0:T(2,128)(2,1)S(1)}, u32[]{:S(2)}, u32[]{:S(2)}) async-start(bf16[8,2,4096]{2,1,0:T(2,128)(2,1)} %reshape.120), calls=%async_computation | async-start | bytes 262144 | tf_op jit(solution)/shard_map/all_to_all | solution.py:31
  27.7 51.3 %all-reduce.3.cloned.1.call-start = ((), (), s32[]{:S(2)}) async-start(), calls=%async_computation.2 | async-start | bytes 524288 | tf_op jit(solution)/shard_map/psum | solution.py:46
  34.0 11.0 %copy-start.1 = (bf16[2,256,512]{2,1,0:T(8,128)(2,1)S(1)}, bf16[2,256,512]{2,1,0:T(8,128)(2,1)}, u32[]{:S(2)}) copy-start(bf16[2,256,512]{2,1,0:T(8,128)(2,1)} %param.13) | copy-start | bytes 1572868
  45.0 34.0 %copy-start.3 = (bf16[2,256,512]{2,1,0:T(8,128)(2,1)S(1)}, bf16[2,256,512]{2,1,0:T(8,128)(2,1)}, u32[]{:S(2)}) copy-start(bf16[2,256,512]{2,1,0:T(8,128)(2,1)} %param.14) | copy-start | bytes 1572868
  45.9 0.7 copy-start.2
  46.0 70.8 %all-reduce.5.cloned.1.call-start = ((), (), s32[]{:S(2)}) async-start(), calls=%async_computation.3 | async-start | bytes 524288 | tf_op jit(solution)/shard_map/psum | solution.py:46
  81.1 52.8 %all-gather.2.cloned.1.call-start = ((), (), s32[]{:S(2)}) async-start(), calls=%async_computation.4 | async-start | bytes 1179648 | tf_op jit(solution)/shard_map/all_gather | solution.py:59
  118.0 16.0 %copy-start.4 = (f32[512]{0:T(512)S(1)}, f32[512]{0:T(512)}, u32[]{:S(2)}) copy-start(f32[512]{0:T(512)} %param.17) | copy-start | bytes 6148
Sparse Core Ops, SparseCore 0:
  46.1 32.8 all-reduce.2
  81.3 35.4 all-reduce.4
Sparse Core Ops, SparseCore 1:
  83.5 23.1 all-gather.1
